TPU v7x, 32 devices: a whole 2x2x4 slice. The times are simulated.
32 devices in a mesh: first: 8 (over z, core), second: 4 (over y, x).
Axes of the slice: x: 2, y: 2, z: 4, core: 2. Of those that a mesh axis runs over, the one named last changes fastest.
Arguments:
- pair_rows: bfloat16 [96, 96, 128], P('first', 'second'), may hold values from -6 to 6
- in_gain: float32 [128], replicated, may hold values from 0.25 to 1.75
- left_weight: bfloat16 [128, 128], replicated, may hold values from -0.5 to 0.5
- right_weight: bfloat16 [128, 128], replicated, may hold values from -0.5 to 0.5
- mid_gain: float32 [128], replicated, may hold values from 0.25 to 1.75
- out_weight: bfloat16 [128, 128], replicated, may hold values from -0.5 to 0.5
- out_gate: bfloat16 [128, 128], replicated, may hold values from -0.5 to 0.5
Outputs:
- triangle_out: bfloat16 [96, 96, 128], P('first', 'second')
All inputs are finite; a program needn't handle non-finite values.
Results may differ from a plain program's by a relative error of at most 0.012.
Values may be sent and summed in bfloat16 or wider, within the bound.
A program may use at most 64 MiB of HBM per device.

v0:
```python
import jax
import jax.numpy as jnp
from jax import lax
from jax.sharding import PartitionSpec as P


def norm_channels(values, channel_gain):
    centred = values - jnp.mean(values, axis=-1, keepdims=True)
    return (
        centred
        * lax.rsqrt(jnp.mean(centred * centred, axis=-1, keepdims=True) + 1e-05)
        * channel_gain
    )


def project_pair(pair_in, in_gain, left_weight, right_weight):
    ready = norm_channels(pair_in.astype(jnp.float32), in_gain).astype(jnp.bfloat16)
    ready = lax.optimization_barrier(ready)
    left = jnp.einsum("ijc,cd->ijd", ready, left_weight, preferred_element_type=jnp.float32)
    right = jnp.einsum("ijc,cd->ijd", ready, right_weight, preferred_element_type=jnp.float32)
    return (ready, left.astype(jnp.bfloat16), right.astype(jnp.bfloat16))


def to_pair(mixed, ready, mid_gain, out_weight, out_gate):
    scaled = norm_channels(mixed.astype(jnp.float32), mid_gain).astype(jnp.bfloat16)
    scaled = lax.optimization_barrier(scaled)
    gate = jax.nn.sigmoid(
        jnp.einsum("ijc,cd->ijd", ready, out_gate, preferred_element_type=jnp.float32)
    )
    return (
        jnp.einsum("ijd,dc->ijc", scaled, out_weight, preferred_element_type=jnp.float32) * gate
    ).astype(jnp.bfloat16)


def shards(pair_rows, in_gain, left_weight, right_weight, mid_gain, out_weight, out_gate):
    ready, left, right = project_pair(pair_rows, in_gain, left_weight, right_weight)
    count = pair_rows.shape[0] * lax.axis_size("first")
    left_lines, right_lines = (
        lax.all_to_all(left, "first", split_axis=2, concat_axis=0, tiled=True),
        lax.all_to_all(right, "first", split_axis=2, concat_axis=0, tiled=True),
    )
    strip = jnp.einsum(
        "kid,kjd->ijd",
        lax.all_gather(left_lines, "second", axis=1, tiled=True),
        right_lines,
        preferred_element_type=jnp.float32,
    )
    strip = (strip * count ** (-0.5)).astype(jnp.bfloat16)
    mixed = lax.all_to_all(strip, "first", split_axis=0, concat_axis=2, tiled=True)
    return to_pair(mixed, ready, mid_gain, out_weight, out_gate)


def solution(mesh):
    in_specs = (P("first", "second", None), P(), P(), P(), P(), P(), P())
    out_specs = P("first", "second", None)
    return jax.shard_map(shards, mesh=mesh, in_specs=in_specs, out_specs=out_specs, check_vma=False)
```

profile of v0, /device:TPU:0, one launch (start us, length us, event | category | flops | bytes accessed | tf_op | source)
XLA Modules:
  0.0 50.4 jit_solution(11390401740638318329)
XLA Ops:
  0.0 1.0 %convert_reduce_fusion = f32[12,24]{1,0:T(8,128)S(1)} fusion(bf16[12,24,128]{2,1,0:T(8,128)(2,1)} %param.7), kind=kLoop, calls=%fused_computation.16 | loop fusion | flops 73440 | bytes 74880 | tf_op jit(solution)/shard_map/reduce_sum | solution.py:8
  1.0 1.1 %fusion.11 = f32[12,24]{1,0:T(8,128)S(1)} fusion(bf16[12,24,128]{2,1,0:T(8,128)(2,1)} %param.7, f32[12,24]{1,0:T(8,128)S(1)} %broadcast_multiply_fusion.1), kind=kLoop, calls=%fused_computation.19 | loop fusion | flops 147168 | bytes 76032 | tf_op jit(solution)/shard_map/reduce_sum | solution.py:11
  2.1 1.0 %fusion.13 = bf16[12,24,128]{2,1,0:T(8,128)(2,1)S(1)} fusion(bf16[12,24,128]{2,1,0:T(8,128)(2,1)} %param.7, f32[128]{0:T(128)} %param.8, f32[12,24]{1,0:T(8,128)S(1)} %add_rsqrt_fusion.1, f32[12,24]{1,0:T(8,128)S(1)} %broadcast_multiply_fusion.1), kind=kLoop, calls=%fused_computation.21 | loop fusion | flops 184320 | bytes 150272 | tf_op jit(solution)/shard_map/convert_element_type | solution.py:17
  3.3 0.4 copy.18
  3.8 1.1 %reshape.41 = bf16[8,2,2304]{2,1,0:T(2,128)(2,1)} reshape(bf16[128,12,24]{2,1,0:T(8,128)(2,1)S(1)} %bitcast.50) | data formatting | bytes 147456
  4.9 6.4 %all-to-all-start = ((bf16[8,2,2304]{2,1,0:T(2,128)(2,1)}), bf16[8,2,2304]{2,1,0:T(2,128)(2,1)S(1)}, u32[]{:S(2)}, u32[]{:S(2)}) async-start(bf16[8,2,2304]{2,1,0:T(2,128)(2,1)} %reshape.41), calls=%async_computation | async-start | bytes 147456 | tf_op jit(solution)/shard_map/all_to_all | solution.py:40
  11.5 0.4 copy.21
  11.9 1.1 %reshape.39 = bf16[8,2,2304]{2,1,0:T(2,128)(2,1)} reshape(bf16[128,12,24]{2,1,0:T(8,128)(2,1)S(1)} %bitcast.51) | data formatting | bytes 147456
  13.0 4.2 %all-to-all-done = bf16[8,2,2304]{2,1,0:T(2,128)(2,1)S(1)} async-done(((bf16[8,2,2304]{2,1,0:T(2,128)(2,1)}), bf16[8,2,2304]{2,1,0:T(2,128)(2,1)S(1)}, u32[]{:S(2)}, u32[]{:S(2)}) %all-to-all-start) | async-done | bytes 73760 | tf_op jit(solution)/shard_map/all_to_all | solution.py:40
  17.2 3.4 %all-to-all-start.1 = ((bf16[8,2,2304]{2,1,0:T(2,128)(2,1)}), bf16[8,2,2304]{2,1,0:T(2,128)(2,1)S(1)}, u32[]{:S(2)}, u32[]{:S(2)}) async-start(bf16[8,2,2304]{2,1,0:T(2,128)(2,1)} %reshape.39), calls=%async_computation.1 | async-start | bytes 147456 | tf_op jit(solution)/shard_map/all_to_all | solution.py:39
  20.6 0.6 %reshape.42 = bf16[128,12,24]{2,1,0:T(8,128)(2,1)S(1)} reshape(bf16[8,2,2304]{2,1,0:T(2,128)(2,1)S(1)} %all-to-all-done) | data formatting | bytes 147456
  21.3 5.2 %all-to-all-done.1 = bf16[8,2,2304]{2,1,0:T(2,128)(2,1)S(1)} async-done(((bf16[8,2,2304]{2,1,0:T(2,128)(2,1)}), bf16[8,2,2304]{2,1,0:T(2,128)(2,1)S(1)}, u32[]{:S(2)}, u32[]{:S(2)}) %all-to-all-start.1) | async-done | bytes 73760 | tf_op jit(solution)/shard_map/all_to_all | solution.py:39
  26.5 0.6 %reshape.40 = bf16[128,12,24]{2,1,0:T(8,128)(2,1)S(1)} reshape(bf16[8,2,2304]{2,1,0:T(2,128)(2,1)S(1)} %all-to-all-done.1) | data formatting | bytes 147456
  27.3 0.4 copy.24
  27.6 10.0 %all_gather.3 = bf16[96,96,16]{0,1,2:T(8,128)(2,1)S(1)} all-gather(bf16[96,24,16]{0,1,2:T(8,128)(2,1)S(1)} %copy.24), channel_id=1, replica_groups=mesh['first'=8,'second'=4] {'second'}, dimensions={1}, use_global_device_ids=true | all-gather | bytes 368640 | tf_op jit(solution)/shard_map/all_gather | solution.py:44
  37.7 0.4 fusion.6
  38.0 0.4 copy.26
  38.4 0.5 reshape.43
  38.9 8.4 %all_to_all.45 = bf16[8,2,2304]{2,1,0:T(2,128)(2,1)S(1)} all-to-all(bf16[8,2,2304]{2,1,0:T(2,128)(2,1)S(1)} %reshape.43), channel_id=1, replica_groups=mesh['first'=8,'second'=4] {'first'}, dimensions={0} | all-to-all | bytes 147456 | tf_op jit(solution)/shard_map/all_to_all | solution.py:49
  47.2 0.5 %reshape.44 = bf16[96,16,24]{2,1,0:T(8,128)(2,1)S(1)} reshape(bf16[8,2,2304]{2,1,0:T(2,128)(2,1)S(1)} %all_to_all.45) | data formatting | bytes 147456
  48.1 0.5 copy.27
  48.6 0.3 reshape.32
  49.1 0.2 copy-done.2
  49.5 0.8 %fusion.5 = bf16[12,24,128]{2,1,0:T(8,128)(2,1)} fusion(f32[12,24,128]{2,1,0:T(8,128)S(1)} %fusion.15, bf16[12,24,128]{2,1,0:T(8,128)(2,1)S(1)} %fusion.13, bf16[128,128]{1,0:T(8,128)(2,1)S(1)} %copy-done.4), kind=kOutput, calls=%fused_computation.7 | convolution fusion | flops 9621504 | bytes 327680 | tf_op jit(solution)/shard_map/ijc,cd->ijd/dot_general | solution.py:28
  (22 shorter events, 1.2 us)
Async XLA Ops:
  0.0 3.2 %copy-start = (bf16[128,128]{1,0:T(8,128)(2,1)S(1)}, bf16[128,128]{1,0:T(8,128)(2,1)}, u32[]{:S(2)}) copy-start(bf16[128,128]{1,0:T(8,128)(2,1)} %param.10) | copy-start | bytes 98308
  0.0 11.3 %copy-start.1 = (bf16[128,128]{1,0:T(8,128)(2,1)S(1)}, bf16[128,128]{1,0:T(8,128)(2,1)}, u32[]{:S(2)}) copy-start(bf16[128,128]{1,0:T(8,128)(2,1)} %param.9) | copy-start | bytes 98308
  4.9 12.3 %all-to-all-start = ((bf16[8,2,2304]{2,1,0:T(2,128)(2,1)}), bf16[8,2,2304]{2,1,0:T(2,128)(2,1)S(1)}, u32[]{:S(2)}, u32[]{:S(2)}) async-start(bf16[8,2,2304]{2,1,0:T(2,128)(2,1)} %reshape.41), calls=%async_computation | async-start | bytes 147456 | tf_op jit(solution)/shard_map/all_to_all | solution.py:40
  17.2 9.3 %all-to-all-start.1 = ((bf16[8,2,2304]{2,1,0:T(2,128)(2,1)}), bf16[8,2,2304]{2,1,0:T(2,128)(2,1)S(1)}, u32[]{:S(2)}, u32[]{:S(2)}) async-start(bf16[8,2,2304]{2,1,0:T(2,128)(2,1)} %reshape.39), calls=%async_computation.1 | async-start | bytes 147456 | tf_op jit(solution)/shard_map/all_to_all | solution.py:39
  48.1 0.8 %copy-start.3 = (f32[128]{0:T(128)S(1)}, f32[128]{0:T(128)}, u32[]{:S(2)}) copy-start(f32[128]{0:T(128)} %param.11) | copy-start | bytes 1540
  48.6 0.8 %copy-start.2 = (bf16[128,128]{1,0:T(8,128)(2,1)S(1)}, bf16[128,128]{1,0:T(8,128)(2,1)}, u32[]{:S(2)}) copy-start(bf16[128,128]{1,0:T(8,128)(2,1)} %param.12) | copy-start | bytes 98308
  48.6 0.9 %copy-start.4 = (bf16[128,128]{1,0:T(8,128)(2,1)S(1)}, bf16[128,128]{1,0:T(8,128)(2,1)}, u32[]{:S(2)}) copy-start(bf16[128,128]{1,0:T(8,128)(2,1)} %param.13) | copy-start | bytes 98308
where the time goes:
time: 50.9 us; the launch traced here: 50.4 us
  blocking collectives  18.4 us (36%)
  starting transfers between devices  9.71 us (19%)
  waiting for transfers between devices  9.4 us (18%)
  local copies, waits for them, and re-layouts  7.34 us (14%)
  other arithmetic  3.56 us (7%)
  matrix products  1.7 us (3%)
    all_gather x1, blocking collectives, shards(): lax.all_gather(left_lines, 'second', axis=1, tiled=True)  10 us
    all_to_all x1, blocking collectives, shards(): lax.all_to_all(strip, 'first', split_axis=0, concat_axis=2, tiled=True)  8.36 us
    all_to_all x1, starting transfers between devices, shards(): lax.all_to_all(right, 'first', split_axis=2, concat_axis=0, tiled=True)  6.35 us
    all_to_all x1, waiting for transfers between devices, shards(): lax.all_to_all(left, 'first', split_axis=2, concat_axis=0, tiled=True)  5.19 us
    unnamed x16, local copies, waits for them, and re-layouts  4.78 us
    all_to_all x1, waiting for transfers between devices, shards(): lax.all_to_all(right, 'first', split_axis=2, concat_axis=0, tiled=True)  4.21 us
    all_to_all x1, starting transfers between devices, shards(): lax.all_to_all(left, 'first', split_axis=2, concat_axis=0, tiled=True)  3.35 us
    reduce_sum x2, other arithmetic, norm_channels(): jnp.mean(centred * centred, axis=-1, keepdims=True) + 1e-05  1.22 us
  transfers between devices with their start and end apart: 2, of which 2 were waited for; matrix products, arithmetic and copies ran while one was open for 5% of the time, Pallas kernels for 0%

commit v1 on v0

v1 whole, which is shorter than its diff:
```python
import functools

import jax
import jax.numpy as jnp
from jax import lax
from jax.experimental import pallas as pl
from jax.experimental.pallas import tpu as pltpu
from jax.sharding import PartitionSpec as P

MESH = pl.DeviceIdType.MESH


def norm_channels(values, channel_gain):
    centred = values - jnp.mean(values, axis=-1, keepdims=True)
    return (
        centred
        * lax.rsqrt(jnp.mean(centred * centred, axis=-1, keepdims=True) + 1e-05)
        * channel_gain
    )


def flip(index, bits, count):
    out, weight = 0, 1
    while weight < count:
        out = out + weight * lax.rem(lax.div(index, weight) + (bits // weight) % 2, 2)
        weight *= 2
    return out


def dot(a, b):
    return jnp.dot(a, b, preferred_element_type=jnp.float32)


def triangle_kernel(
    rows, cols, planes, lines,
    x_ref, in_gain_ref, left_w_ref, right_w_ref, mid_gain_ref, out_w_ref, gate_w_ref,
    out_ref,
    split, lsend, lrecv, rsend, rrecv, left32, right32, own, psend, precv, gate,
    lsend_sem, lrecv_sem, rsend_sem, rrecv_sem, psend_sem, precv_sem,
):
    first, second = lax.axis_index("first"), lax.axis_index("second")
    z, core = lax.div(first, 2), lax.rem(first, 2)
    pairs = rows * cols
    half = cols // 2

    def device(z_at, core_at, second_at):
        return {"first": 2 * z_at + core_at, "second": second_at}

    barrier = pltpu.get_barrier_semaphore()
    peers = 0
    for t in range(lines):
        for rel in range(2):
            if t or rel:
                to = device(z, lax.rem(core + rel, 2), flip(second, t, lines))
                pl.semaphore_signal(barrier, inc=1, device_id=to, device_id_type=MESH)
                peers += 1
    for dz in range(1, planes):
        to = device(lax.rem(z + dz, planes), core, second)
        pl.semaphore_signal(barrier, inc=1, device_id=to, device_id_type=MESH)
        peers += 1

    ready = norm_channels(x_ref[...].astype(jnp.float32), in_gain_ref[...]).astype(jnp.bfloat16)
    left = dot(ready, left_w_ref[...])
    for k in range(rows):
        for h in range(2):
            at = k * cols + h * half
            split[h, k * half : (k + 1) * half, :] = left[at : at + half, :]
    for h in range(2):
        lsend[h] = split[h].astype(jnp.bfloat16)
    right = dot(ready, right_w_ref[...]).astype(jnp.bfloat16)
    rsend[...] = right

    pl.semaphore_wait(barrier, peers)

    left_copies = {}
    for t in range(lines - 1, -1, -1):
        for rel in range(2):
            if t or rel:
                to_core = lax.rem(core + rel, 2)
                copy = pltpu.make_async_remote_copy(
                    src_ref=lsend.at[to_core],
                    dst_ref=lrecv.at[t, rel],
                    send_sem=lsend_sem.at[t, rel],
                    recv_sem=lrecv_sem.at[t, rel],
                    device_id=device(z, to_core, flip(second, t, lines)),
                    device_id_type=MESH,
                )
                copy.start()
                left_copies[t, rel] = copy
    right_copy = pltpu.make_async_remote_copy(
        src_ref=rsend,
        dst_ref=rrecv,
        send_sem=rsend_sem,
        recv_sem=rrecv_sem,
        device_id=device(z, 1 - core, second),
        device_id_type=MESH,
    )
    right_copy.start()

    gate[...] = jax.nn.sigmoid(dot(ready, gate_w_ref[...]))
    right32[0] = right.astype(jnp.float32)
    right_copy.wait_recv()
    right32[1] = rrecv[...].astype(jnp.float32)

    part_copies = []
    for t in range(lines):
        for rel in range(2):
            if t or rel:
                left_copies[t, rel].wait_recv()
                left32[rel] = lrecv[t, rel].astype(jnp.float32)
            else:
                left32[rel] = lsend[core].astype(jnp.float32)

        sums = tuple(jnp.zeros((cols, x_ref.shape[1]), jnp.float32) for _ in range(half))
        for rel in range(2):

            def body(k, sums):
                r = right32[rel, pl.ds(pl.multiple_of(k * cols, 8), cols), :]
                return tuple(
                    total + left32[rel, pl.ds(k * half + i, 1), :] * r
                    for i, total in enumerate(sums)
                )

            sums = lax.fori_loop(0, rows, body, sums)

        z_to = flip(second, t, lines)
        is_own = z_to == z

        @pl.when(is_own)
        def _():
            for i, total in enumerate(sums):
                own[i * cols : (i + 1) * cols, :] = total

        for i in range(0, half, 2):
            two = jnp.concatenate([sums[i], sums[i + 1]], axis=0)
            psend[t, i * cols : (i + 2) * cols, :] = two.astype(jnp.bfloat16)
        slot = lax.rem(z - z_to + 2 * planes - 1, planes)
        copy = pltpu.make_async_remote_copy(
            src_ref=psend.at[t],
            dst_ref=precv.at[slot],
            send_sem=psend_sem.at[t],
            recv_sem=precv_sem.at[slot],
            device_id=device(z_to, core, second),
            device_id_type=MESH,
        )
        part_copies.append((is_own, copy))

        @pl.when(jnp.logical_not(is_own))
        def _():
            copy.start()

    total = own[...]
    for slot in range(planes - 1):
        pltpu.make_async_remote_copy(
            src_ref=psend.at[0],
            dst_ref=precv.at[slot],
            send_sem=psend_sem.at[0],
            recv_sem=precv_sem.at[slot],
            device_id=device(lax.rem(z + 1, planes), core, second),
            device_id_type=MESH,
        ).wait_recv()
        total = total + precv[slot].astype(jnp.float32)
    count = rows * 2 * planes
    mixed = (total * count ** (-0.5)).astype(jnp.bfloat16)
    scaled = norm_channels(mixed.astype(jnp.float32), mid_gain_ref[...]).astype(jnp.bfloat16)
    out_ref[...] = (dot(scaled, out_w_ref[...]) * gate[...]).astype(jnp.bfloat16)

    for copy in left_copies.values():
        copy.wait_send()
    right_copy.wait_send()
    for is_own, copy in part_copies:

        @pl.when(jnp.logical_not(is_own))
        def _():
            copy.wait_send()


def triangle(planes, lines, pair_rows, in_gain, left_weight, right_weight, mid_gain, out_weight, out_gate):
    rows, cols, width = pair_rows.shape
    mix = left_weight.shape[1]
    pairs, half = rows * cols, cols // 2
    vmem = pl.BlockSpec(memory_space=pltpu.VMEM)
    bf16, f32 = jnp.bfloat16, jnp.float32
    out = pl.pallas_call(
        functools.partial(triangle_kernel, rows, cols, planes, lines),
        out_shape=jax.ShapeDtypeStruct((pairs, width), bf16),
        in_specs=[vmem] * 7,
        out_specs=vmem,
        scratch_shapes=[
            pltpu.VMEM((2, rows * half, mix), f32),
            pltpu.VMEM((2, rows * half, mix), bf16),
            pltpu.VMEM((lines, 2, rows * half, mix), bf16),
            pltpu.VMEM((pairs, mix), bf16),
            pltpu.VMEM((pairs, mix), bf16),
            pltpu.VMEM((2, rows * half, mix), f32),
            pltpu.VMEM((2, pairs, mix), f32),
            pltpu.VMEM((half * cols, mix), f32),
            pltpu.VMEM((lines, half * cols, mix), bf16),
            pltpu.VMEM((planes - 1, half * cols, mix), bf16),
            pltpu.VMEM((pairs, width), f32),
            pltpu.SemaphoreType.DMA((lines, 2)),
            pltpu.SemaphoreType.DMA((lines, 2)),
            pltpu.SemaphoreType.DMA,
            pltpu.SemaphoreType.DMA,
            pltpu.SemaphoreType.DMA((lines,)),
            pltpu.SemaphoreType.DMA((planes - 1,)),
        ],
        compiler_params=pltpu.CompilerParams(collective_id=0, has_side_effects=True),
    )(
        pair_rows.reshape(pairs, width), in_gain.reshape(1, width), left_weight, right_weight,
        mid_gain.reshape(1, mix), out_weight, out_gate,
    )
    return out.reshape(rows, cols, width)


def shards(pair_rows, in_gain, left_weight, right_weight, mid_gain, out_weight, out_gate):
    ready = norm_channels(pair_rows.astype(jnp.float32), in_gain).astype(jnp.bfloat16)
    ready = lax.optimization_barrier(ready)
    left = jnp.einsum("ijc,cd->ijd", ready, left_weight, preferred_element_type=jnp.float32)
    right = jnp.einsum("ijc,cd->ijd", ready, right_weight, preferred_element_type=jnp.float32)
    left, right = left.astype(jnp.bfloat16), right.astype(jnp.bfloat16)
    count = pair_rows.shape[0] * lax.axis_size("first")
    left_lines, right_lines = (
        lax.all_to_all(left, "first", split_axis=2, concat_axis=0, tiled=True),
        lax.all_to_all(right, "first", split_axis=2, concat_axis=0, tiled=True),
    )
    strip = jnp.einsum(
        "kid,kjd->ijd",
        lax.all_gather(left_lines, "second", axis=1, tiled=True),
        right_lines,
        preferred_element_type=jnp.float32,
    )
    strip = (strip * count ** (-0.5)).astype(jnp.bfloat16)
    mixed = lax.all_to_all(strip, "first", split_axis=0, concat_axis=2, tiled=True)
    scaled = norm_channels(mixed.astype(jnp.float32), mid_gain).astype(jnp.bfloat16)
    scaled = lax.optimization_barrier(scaled)
    gate = jax.nn.sigmoid(
        jnp.einsum("ijc,cd->ijd", ready, out_gate, preferred_element_type=jnp.float32)
    )
    return (
        jnp.einsum("ijd,dc->ijc", scaled, out_weight, preferred_element_type=jnp.float32) * gate
    ).astype(jnp.bfloat16)


def solution(mesh):
    in_specs = (P("first", "second", None), P(), P(), P(), P(), P(), P())
    out_specs = P("first", "second", None)
    planes, lines = mesh.shape["first"] // 2, mesh.shape["second"]
    if mesh.shape["first"] == 2 * lines and lines & (lines - 1) == 0:
        body = functools.partial(triangle, planes, lines)
    else:
        body = shards
    return jax.shard_map(body, mesh=mesh, in_specs=in_specs, out_specs=out_specs, check_vma=False)
```

time: 50.9 us -> 20.6 us (0.40)
  the two profiles are of different devices: /device:TPU:0 before, /device:TPU:6 now
where the time goes in v1:
time: 20.6 us; the launch traced here: 20.4 us
  Pallas kernels  18.9 us (92%)
  local copies, waits for them, and re-layouts  1.52 us (7%)
    pallas_call x1, Pallas kernels, triangle(): pl.pallas_call(functools.partial(triangle_kernel, rows, cols, planes, lin...  18.9 us
    unnamed x1, local copies, waits for them, and re-layouts  1.52 us

profile of v1, /device:TPU:6, one launch (start us, length us, event | category | flops | bytes accessed | tf_op | source)
XLA Modules:
  0.0 20.4 jit_solution(268367610929308448)
XLA Ops:
  0.0 18.9 %shard_map.73 = bf16[288,128]{1,0:T(8,128)(2,1)} custom-call(bf16[288,128]{1,0:T(8,128)(2,1)} %bitcast.5, f32[1,128]{1,0:T(1,128)} %bitcast.6, bf16[128,128]{1,0:T(8,128)(2,1)} %left_w_ref.1, bf16[128,128]{1,0:T(8,128)(2,1)} %right_w_ref.1, f32[1,128]{1,0:T(1,128)} %bitcast.7, bf16[128,128]{1,0:T(8,128)(2,1)} %out_w_ref.1, bf16[128,128]{1,0:T(8,128)(2,1)} %gate_w_ref.1), custom_call_target="tpu_custom_call" | custom-call | tf_op jit(solution)/shard_map/pallas_call | solution.py:184
  18.9 1.5 %copy.9 = bf16[12,24,128]{2,1,0:T(8,128)(2,1)} copy(bf16[12,24,128]{2,1,0:T(8,128)(2,1)} %bitcast.4) | data formatting | bytes 147456
